TPU v7x, 32 devices: a whole 2x2x4 slice. The times are simulated.
32 devices in a mesh: seq: 4 (over y, x), tp: 4 (over z), grp: 2 (over core).
Axes of the slice: x: 2, y: 2, z: 4, core: 2. Of those that a mesh axis runs over, the one named last changes fastest.
Arguments:
- query: bfloat16 [16, 64, 8192], P('grp', None, 'tp'), parts along dimension 0, may hold values from -15 to 15
- cache: bfloat16 [16, 4096, 8, 256], P('grp', 'tp', 'seq'), parts along dimension 0, may hold values from -6 to 6
- head_of_slot: int32 [16], P('grp'), parts along dimension 0, may hold values from 0 to 7, each once
- lengths: int32 [16], P('grp'), parts along dimension 0, may hold values from 2048 to 4096
- out_weight: bfloat16 [8192, 8192], P('tp', 'seq'), may hold values from -0.0625 to 0.0625
Outputs:
- projected: bfloat16 [16, 64, 8192], P(('grp', 'tp'), None, 'seq'), parts along dimension 0
There are 2 independent parts, one for each index of `grp`. A program takes and returns all parts, laid end to end along the dimension named above; an argument that names none is the same for every part. Nothing has to cross between parts.
Inputs may be any that keep to these rules, and one draw needn't show every extreme that they name: head_of_slot names every KV head exactly once.
All inputs are finite; a program needn't handle non-finite values.
Results may differ from a plain program's by a relative error of at most 0.01.
Values may be sent and summed in bfloat16 or wider, within the bound.
A program may use at most 128 MiB of HBM per device.

v0:
```python
import math

import jax
import jax.numpy as jnp
from jax import lax
from jax.sharding import PartitionSpec as P

HQ = 64
KVH = 8


MASKED_SCORE = -1e30


def merged(shard, axis, combine):
    everything = jax.tree.map(lambda part: lax.all_gather(part, axis), shard)
    first = jax.tree.map(lambda part: part[0], everything)

    def step(k, so_far):
        return combine(so_far, jax.tree.map(lambda part: part[k], everything))

    return lax.fori_loop(1, lax.axis_size(axis), step, first)


def slot_table(head_of_slot):
    slot_total = head_of_slot.shape[0]
    slot_ids = jnp.arange(slot_total, dtype=jnp.int32)
    return jnp.sum(
        jnp.where(head_of_slot[None, :] == slot_ids[:, None], slot_ids[None, :], 0), axis=1
    )


def combine(earlier, latter):
    maxima = jnp.maximum(earlier[0], latter[0])
    early_scale = jnp.exp(earlier[0] - maxima)
    late_scale = jnp.exp(latter[0] - maxima)
    totals = earlier[1] * early_scale + latter[1] * late_scale
    blended = earlier[2] * early_scale[..., None] + latter[2] * late_scale[..., None]
    return (maxima, totals, blended)


def partial_attention(queries, entries, positions, lengths, group_size):
    seq_total, tokens = (queries.shape[0], queries.shape[1])
    head_count = entries.shape[2]
    head_dim = entries.shape[3] // 2
    row_count = tokens * group_size
    stacked = queries.reshape(seq_total, tokens, head_count, group_size, head_dim)
    stacked = stacked.transpose(0, 2, 1, 3, 4).reshape(seq_total, head_count, row_count, head_dim)
    limits = (
        lengths[:, None] - tokens + jnp.arange(row_count, dtype=jnp.int32)[None, :] // group_size
    )
    scaling = 1.0 / math.sqrt(head_dim)
    extent = entries.shape[1]
    block_len = math.gcd(extent, 512)

    def advance(turn_index, carried):
        maxima, totals, blended = carried
        first_pos = turn_index * block_len
        entry_block = lax.dynamic_slice_in_dim(entries, first_pos, block_len, 1)
        block_pos = lax.dynamic_slice_in_dim(positions, first_pos, block_len, 0)
        scores = (
            jnp.einsum(
                "bnrd,bknd->bnrk",
                stacked,
                entry_block[..., :head_dim],
                preferred_element_type=jnp.float32,
            )
            * scaling
        )
        visible = block_pos[None, None, None, :] <= limits[:, None, :, None]
        scores = jnp.where(visible, scores, MASKED_SCORE)
        new_max = jnp.maximum(maxima, jnp.max(scores, axis=3))
        shrink = jnp.exp(maxima - new_max)
        weights = jnp.where(visible, jnp.exp(scores - new_max[..., None]), 0.0)
        totals = totals * shrink + jnp.sum(weights, axis=3)
        blended = blended * shrink[..., None] + jnp.einsum(
            "bnrk,bknd->bnrd",
            weights.astype(jnp.bfloat16),
            entry_block[..., head_dim:],
            preferred_element_type=jnp.float32,
        )
        return (new_max, totals, blended)

    initial = (
        jnp.full((seq_total, head_count, row_count), MASKED_SCORE, jnp.float32),
        jnp.zeros((seq_total, head_count, row_count), jnp.float32),
        jnp.zeros((seq_total, head_count, row_count, head_dim), jnp.float32),
    )
    return lax.fori_loop(0, extent // block_len, advance, initial)


def normalize(totals, blended, tokens, group_size):
    seq_total, head_count, row_count, head_dim = blended.shape
    attended = (blended / totals[..., None]).astype(jnp.bfloat16)
    attended = attended.reshape(seq_total, head_count, tokens, group_size, head_dim).transpose(
        0, 2, 1, 3, 4
    )
    return attended.reshape(seq_total, tokens, head_count * group_size * head_dim)


def local(query, cache, head_of_slot, lengths, out_weight):
    group_size = HQ // KVH
    seq_devices = lax.axis_size("seq")
    tp_devices = lax.axis_size("tp")
    seq_rank = lax.axis_index("seq")
    slot_of_head = slot_table(head_of_slot)
    seq_total, tokens = (query.shape[0], query.shape[1])
    regrouped = lax.all_to_all(cache, "seq", split_axis=1, concat_axis=2, tiled=True)
    extent = regrouped.shape[1]
    by_head = jnp.take(regrouped, slot_of_head, axis=2)
    owned = lax.all_to_all(by_head, "tp", split_axis=2, concat_axis=1, tiled=True)
    local_rows = jnp.arange(owned.shape[1], dtype=jnp.int32)
    positions = (
        local_rows // extent * (extent * seq_devices) + seq_rank * extent + local_rows % extent
    )
    partials = partial_attention(query, owned, positions, lengths, group_size)
    maxima, totals, blended = merged(partials, "seq", combine)
    attended = normalize(totals, blended, tokens, group_size)
    flattened = attended.reshape(seq_total * tokens, attended.shape[2])
    summed = lax.psum_scatter(
        jnp.dot(flattened, out_weight, preferred_element_type=jnp.float32),
        "tp",
        scatter_dimension=0,
        tiled=True,
    )
    return summed.astype(jnp.bfloat16).reshape(seq_total // tp_devices, tokens, summed.shape[1])


def solution(mesh):
    in_specs = (
        P("grp", None, "tp"),
        P("grp", "tp", "seq", None),
        P("grp"),
        P("grp"),
        P("tp", "seq"),
    )
    out_specs = P(("grp", "tp"), None, "seq")
    return jax.shard_map(local, mesh=mesh, in_specs=in_specs, out_specs=out_specs, check_vma=False)
```

profile of v0, /device:TPU:28, one launch (start us, length us, event | category | flops | bytes accessed | tf_op | source)
XLA Modules:
  0.0 702.4 jit_solution(4291762971954371989)
XLA Ops:
  6.5 8.1 %copy.31 = bf16[8,1024,2,256]{3,2,0,1:T(2,128)(2,1)} copy(bf16[8,1024,2,256]{3,2,1,0:T(2,128)(2,1)} %param.10) | data formatting | bytes 16777216 | tf_op args[1]
  14.6 6.3 all-to-all-start
  21.1 92.0 %all-to-all-done = bf16[8,1024,2,256]{3,2,0,1:T(2,128)(2,1)} async-done(((bf16[8,1024,2,256]{3,2,0,1:T(2,128)(2,1)}), bf16[8,1024,2,256]{3,2,0,1:T(2,128)(2,1)}, u32[]{:S(2)}, u32[]{:S(2)}) %all-to-all-start) | async-done | bytes 8388640 | tf_op jit(solution)/shard_map/all_to_all | solution.py:108
  113.0 9.6 %copy.32 = bf16[8,1024,2,256]{3,1,2,0:T(8,128)(2,1)} copy(bf16[8,1024,2,256]{3,2,0,1:T(2,128)(2,1)} %all-to-all-done) | data formatting | bytes 16777216 | tf_op jit(solution)/shard_map/all_to_all | solution.py:108
  122.6 7.6 %copy.33 = bf16[8,256,4,2,256]{4,1,3,2,0:T(8,128)(2,1)} copy(bf16[8,256,4,2,256]{4,1,2,3,0:T(8,128)(2,1)} %bitcast.78) | data formatting | bytes 16777216 | tf_op jit(solution)/shard_map/all_to_all | solution.py:108
  130.2 7.6 %copy.34 = bf16[8,256,8,256]{3,1,0,2:T(8,128)(2,1)} copy(bf16[8,256,8,256]{3,1,2,0:T(8,128)(2,1)} %bitcast.79) | data formatting | bytes 16777216 | tf_op jit(solution)/shard_map/all_to_all | solution.py:108
  137.8 8.1 %gather_fusion = bf16[8,8,256,256]{3,2,1,0:T(8,128)(2,1)} fusion(bf16[8,256,8,256]{3,1,0,2:T(8,128)(2,1)} %copy.34, s32[1024]{0:T(1024)S(1)} %pad_clamp_fusion), kind=kCustom, calls=%fused_computation | custom fusion | bytes 16777248 | tf_op jit(solution)/shard_map/jit(_take)/gather | solution.py:110
  145.9 7.5 %select_bitcast_fusion = bf16[8,256,8,256]{3,1,0,2:T(8,128)(2,1)} fusion(bf16[8,8,256,256]{3,2,1,0:T(8,128)(2,1)} %gather_fusion, pred[8]{0:T(512)(128)(4,1)S(1)} %compare_and_fusion), kind=kLoop, calls=%fused_computation.34 | loop fusion | flops 4194304 | bytes 16777224 | tf_op jit(solution)/shard_map/jit(_take)/select_n | solution.py:110
  153.4 5.8 all-to-all-start.1
  160.1 1.8 copy.44
  161.9 177.7 %all-to-all-done.1 = bf16[8,256,8,256]{3,1,0,2:T(8,128)(2,1)} async-done(((bf16[8,256,8,256]{3,1,0,2:T(8,128)(2,1)}), bf16[8,256,8,256]{3,1,0,2:T(8,128)(2,1)}, u32[]{:S(2)}, u32[]{:S(2)}) %all-to-all-start.1) | async-done | bytes 8388640 | tf_op jit(solution)/shard_map/all_to_all | solution.py:111
  339.6 7.6 %copy.36 = bf16[8,4,256,2,256]{4,2,1,3,0:T(8,128)(2,1)} copy(bf16[8,4,256,2,256]{4,2,0,3,1:T(8,128)(2,1)} %bitcast.11) | data formatting | bytes 16777216 | tf_op jit(solution)/shard_map/all_to_all | solution.py:111
  347.2 67.7 %while.38 = (s32[]{:T(128)}, f32[8,2,512]{2,1,0:T(2,128)S(1)}, f32[8,2,512]{2,1,0:T(2,128)S(1)}, f32[8,2,512,128]{3,2,1,0:T(8,128)}, s32[1024]{0:T(1024)S(1)}, /...) while((s32[]{:T(128)}, f32[8,2,512]{2,1,0:T(2,128)S(1)}, ...), condition=%wide.region_4.5_spmd.clone, body=%wide.region_1.0_spmd.clone.sunk | while | flops 2207297536 | bytes 73965816 | solution.py:89
  348.6 11.5 %fusion.62 = (f32[8,2,512]{2,1,0:T(2,128)S(1)}, f32[8,2,512,512]{3,2,1,0:T(8,128)}) fusion(pred[8,512,512]{1,2,0:T(8,128)(4,1)S(1)} %broadcast_compare_fusion.2, bf16[8,2,512,128]{3,2,1,0:T(8,128)(2,1)} %get-tuple-element.550, bf16[8,1024,2,256]{3,1,2,0:T(8,128)(2,1)} %get-tuple-element.549, s32[]{:T(128)S(6)} %select_n.144), kind=kOutput, calls=%fused_computation.12.clone.1 | convolution fusion | flops 1086316544 | bytes 23101444 | tf_op jit(solution)/shard_map/while/body/eval_jaxpr/bnrd,bknd->bnrk/dot_general | solution.py:62
  360.2 8.1 %fusion.64 = f32[8,2,512]{2,1,0:T(2,128)S(1)} fusion(f32[8,2,512,512]{3,2,1,0:T(8,128)} %get-tuple-element.513, f32[8,2,512]{2,1,0:T(2,128)S(1)} %fusion.63, pred[8,512,512]{1,2,0:T(8,128)(4,1)S(1)} %broadcast_compare_fusion.2), kind=kLoop, calls=%fused_computation.14.clone.1 | loop fusion | flops 20963328 | bytes 18939904 | tf_op jit(solution)/shard_map/while/body/eval_jaxpr/reduce_sum | solution.py:75
  368.4 12.4 %fusion.66 = f32[8,2,512,128]{3,2,1,0:T(8,128)} fusion(f32[8,2,512,128]{3,2,1,0:T(8,128)} %get-tuple-element.533, f32[8,2,512]{2,1,0:T(2,128)S(1)} %get-tuple-element.515, pred[]{:T(512)S(6)} %compare.12, bf16[8,1024,2,256]{3,1,2,0:T(8,128)(2,1)} %get-tuple-element.549, s32[]{:T(128)S(6)} %select_n.144, s32[]{:T(128)S(6)} %add.219, ...), kind=kOutput, calls=%fused_computation.18.clone.1 | convolution fusion | flops 1097859072 | bytes 29425672 | tf_op jit(solution)/shard_map/while/body/eval_jaxpr/bnrk,bknd->bnrd/dot_general | solution.py:76
  382.2 11.5 %fusion.62 = (f32[8,2,512]{2,1,0:T(2,128)S(1)}, f32[8,2,512,512]{3,2,1,0:T(8,128)}) fusion(pred[8,512,512]{1,2,0:T(8,128)(4,1)S(1)} %broadcast_compare_fusion.2, bf16[8,2,512,128]{3,2,1,0:T(8,128)(2,1)} %get-tuple-element.550, bf16[8,1024,2,256]{3,1,2,0:T(8,128)(2,1)} %get-tuple-element.549, s32[]{:T(128)S(6)} %select_n.144), kind=kOutput, calls=%fused_computation.12.clone.1 | convolution fusion | flops 1086316544 | bytes 23101444 | tf_op jit(solution)/shard_map/while/body/eval_jaxpr/bnrd,bknd->bnrk/dot_general | solution.py:62
  393.7 8.1 %fusion.64 = f32[8,2,512]{2,1,0:T(2,128)S(1)} fusion(f32[8,2,512,512]{3,2,1,0:T(8,128)} %get-tuple-element.513, f32[8,2,512]{2,1,0:T(2,128)S(1)} %fusion.63, pred[8,512,512]{1,2,0:T(8,128)(4,1)S(1)} %broadcast_compare_fusion.2), kind=kLoop, calls=%fused_computation.14.clone.1 | loop fusion | flops 20963328 | bytes 18939904 | tf_op jit(solution)/shard_map/while/body/eval_jaxpr/reduce_sum | solution.py:75
  401.9 13.0 %fusion.66 = f32[8,2,512,128]{3,2,1,0:T(8,128)} fusion(f32[8,2,512,128]{3,2,1,0:T(8,128)} %get-tuple-element.533, f32[8,2,512]{2,1,0:T(2,128)S(1)} %get-tuple-element.515, pred[]{:T(512)S(6)} %compare.12, bf16[8,1024,2,256]{3,1,2,0:T(8,128)(2,1)} %get-tuple-element.549, s32[]{:T(128)S(6)} %select_n.144, s32[]{:T(128)S(6)} %add.219, ...), kind=kOutput, calls=%fused_computation.18.clone.1 | convolution fusion | flops 1097859072 | bytes 29425672 | tf_op jit(solution)/shard_map/while/body/eval_jaxpr/bnrk,bknd->bnrd/dot_general | solution.py:76
  415.0 7.6 %all-gather = f32[32,2,512]{2,1,0:T(2,128)S(1)} all-gather(f32[8,2,512]{2,1,0:T(2,128)S(1)} %get-tuple-element.323), channel_id=2, replica_groups=mesh['seq'=4,'tp'=4,'grp'=2] {'seq'}, dimensions={0}, use_global_device_ids=true | all-gather | bytes 163840 | tf_op jit(solution)/shard_map/all_gather | solution.py:16
  422.6 9.4 %all-gather.1 = f32[32,2,512]{2,1,0:T(2,128)S(1)} all-gather(f32[8,2,512]{2,1,0:T(2,128)S(1)} %get-tuple-element.324), channel_id=3, replica_groups=mesh['seq'=4,'tp'=4,'grp'=2] {'seq'}, dimensions={0}, use_global_device_ids=true | all-gather | bytes 163840 | tf_op jit(solution)/shard_map/all_gather | solution.py:16
  432.0 140.8 %all-gather.5.cloned.1.call-done = f32[32,2,512,128]{3,2,1,0:T(8,128)} async-done(((f32[8,2,512,128]{3,2,1,0:T(8,128)}), f32[32,2,512,128]{3,2,1,0:T(8,128)}) %all-gather.5.cloned.1.call-update) | async-done | bytes 16777232 | tf_op jit(solution)/shard_map/all_gather | solution.py:16
  572.7 4.5 slice.35
  577.3 24.1 %while.37 = (s32[]{:T(128)}, f32[8,2,512]{2,1,0:T(2,128)S(1)}, f32[8,2,512]{2,1,0:T(2,128)S(1)}, f32[8,2,512,128]{3,2,1,0:T(8,128)}, f32[4,8,2,512]{3,2,1,0:T(2,...) while((s32[]{:T(128)}, f32[8,2,512]{2,1,0:T(2,128)S(1)}, ...), condition=%wide.region_6.7_spmd, body=%wide.region_5.6_spmd.sunk | while | flops 3194885 | bytes 12910743 | solution.py:22
  577.3 8.0 %fusion.58 = f32[8,2,512,128]{3,2,1,0:T(8,128)} fusion(f32[4,8,2,512,128]{4,3,2,1,0:T(8,128)} %get-tuple-element.584, s32[]{:T(128)S(6)} %select_n.138, f32[8,2,512,128]{3,2,1,0:T(8,128)} %get-tuple-element.571, f32[8,2,512]{2,1,0:T(2,128)S(1)} %get-tuple-element.501, f32[8,2,512]{2,1,0:T(2,128)S(1)} %get-tuple-element.502), kind=kLoop, calls=%fused_computation.3.clone.1 | loop fusion | flops 3145728 | bytes 12648452 | tf_op jit(solution)/shard_map/while/body/eval_jaxpr/add | solution.py:38
  585.4 8.0 %fusion.58 = f32[8,2,512,128]{3,2,1,0:T(8,128)} fusion(f32[4,8,2,512,128]{4,3,2,1,0:T(8,128)} %get-tuple-element.584, s32[]{:T(128)S(6)} %select_n.138, f32[8,2,512,128]{3,2,1,0:T(8,128)} %get-tuple-element.571, f32[8,2,512]{2,1,0:T(2,128)S(1)} %get-tuple-element.501, f32[8,2,512]{2,1,0:T(2,128)S(1)} %get-tuple-element.502), kind=kLoop, calls=%fused_computation.3.clone.1 | loop fusion | flops 3145728 | bytes 12648452 | tf_op jit(solution)/shard_map/while/body/eval_jaxpr/add | solution.py:38
  593.4 8.0 %fusion.58 = f32[8,2,512,128]{3,2,1,0:T(8,128)} fusion(f32[4,8,2,512,128]{4,3,2,1,0:T(8,128)} %get-tuple-element.584, s32[]{:T(128)S(6)} %select_n.138, f32[8,2,512,128]{3,2,1,0:T(8,128)} %get-tuple-element.571, f32[8,2,512]{2,1,0:T(2,128)S(1)} %get-tuple-element.501, f32[8,2,512]{2,1,0:T(2,128)S(1)} %get-tuple-element.502), kind=kLoop, calls=%fused_computation.3.clone.1 | loop fusion | flops 3145728 | bytes 12648452 | tf_op jit(solution)/shard_map/while/body/eval_jaxpr/add | solution.py:38
  601.4 2.9 copy_bitcast_fusion
  604.2 2.3 reshape_reshape.3
  606.5 10.5 %fusion.42 = f32[512,2048]{1,0:T(8,128)} fusion(bf16[512,2048]{1,0:T(8,128)(2,1)} %reshape_reshape.3, bf16[2048,2048]{1,0:T(8,128)(2,1)} %param.13), kind=kOutput, calls=%fused_computation.68 | convolution fusion | flops 4294967296 | bytes 14680064 | tf_op jit(solution)/shard_map/dot_general | solution.py:121
  617.0 76.4 %reduce-scatter.2.cloned.1.call-done = f32[128,2048]{1,0:T(8,128)} async-done(((f32[512,2048]{1,0:T(8,128)}), f32[128,2048]{1,0:T(8,128)}) %reduce-scatter.2.cloned.1.call-update) | async-done | bytes 1048592 | tf_op jit(solution)/shard_map/reduce_scatter | solution.py:120
  693.5 2.1 convert_element_type.14
  (38 shorter events, 4.4 us)
Async XLA Ops:
  14.6 6.3 copy-start.1
  14.6 98.4 %all-to-all-start = ((bf16[8,1024,2,256]{3,2,0,1:T(2,128)(2,1)}), bf16[8,1024,2,256]{3,2,0,1:T(2,128)(2,1)}, u32[]{:S(2)}, u32[]{:S(2)}) async-start(bf16[8,1024,2,256]{3,2,0,1:T(2,128)(2,1)} %copy.31), calls=%async_computation | async-start | bytes 16777216 | tf_op jit(solution)/shard_map/all_to_all | solution.py:108
  153.4 6.1 copy-start
  153.4 186.2 %all-to-all-start.1 = ((bf16[8,256,8,256]{3,1,0,2:T(8,128)(2,1)}), bf16[8,256,8,256]{3,1,0,2:T(8,128)(2,1)}, u32[]{:S(2)}, u32[]{:S(2)}) async-start(bf16[8,256,8,256]{3,1,0,2:T(8,128)(2,1)} %select_bitcast_fusion), calls=%async_computation.1 | async-start | bytes 16777216 | tf_op jit(solution)/shard_map/all_to_all | solution.py:111
  159.2 2.7 copy-start.2
  159.2 413.6 %all-gather.5.cloned.1.call-start = ((), (), s32[]{:S(2)}) async-start(), calls=%async_computation.4 | async-start | bytes 20971520 | tf_op jit(solution)/shard_map/all_gather | solution.py:16
  414.9 278.5 %reduce-scatter.2.cloned.1.call-start = ((), (), s32[]{:S(2)}) async-start(), calls=%async_computation.3 | async-start | bytes 5242880 | tf_op jit(solution)/shard_map/reduce_scatter | solution.py:120
Sparse Core Ops, SparseCore 0:
  415.1 157.6 all-gather.4
  617.1 76.2 reduce-scatter.1
where the time goes:
time: 706 us; the launch traced here: 702 us
  waiting for transfers between devices  487 us (69%)
  matrix products  58.8 us (8%)
  local copies, waits for them, and re-layouts  58 us (8%)
  other arithmetic  55.8 us (8%)
  blocking collectives  17 us (2%)
  between operations  13.5 us (2%)
  starting transfers between devices  12.3 us (2%)
    all_to_all x1, waiting for transfers between devices, local(): lax.all_to_all(by_head, 'tp', split_axis=2, concat_axis=1, tiled=True)  178 us
    all_gather x1, waiting for transfers between devices, merged(): everything = jax.tree.map(lambda part: lax.all_gather(part, axis), shard)  141 us
    all_to_all x1, waiting for transfers between devices, local(): lax.all_to_all(cache, 'seq', split_axis=1, concat_axis=2, tiled=True)  92 us
    reduce_scatter x1, waiting for transfers between devices, local(): lax.psum_scatter(jnp.dot(flattened, out_weight, preferred_element_type=jn...  76.4 us
    dot_general x2, matrix products, advance(): jnp.einsum('bnrk,bknd->bnrd', weights.astype(jnp.bfloat16), entry_block[....  25.4 us
    all_to_all x3, local copies, waits for them, and re-layouts, local(): lax.all_to_all(cache, 'seq', split_axis=1, concat_axis=2, tiled=True)  24.8 us
    add x3, other arithmetic, combine(): earlier[2] * early_scale[..., None] + latter[2] * late_scale[..., None]  23.9 us
    dot_general x2, matrix products, advance(): jnp.einsum('bnrd,bknd->bnrk', stacked, entry_block[..., :head_dim], prefe...  23 us
  transfers between devices with their start and end apart: 4, of which 4 were waited for; matrix products, arithmetic and copies ran while one was open for 0% of the time, Pallas kernels for 0%

commit v1 on v0

v1 whole, which is shorter than its diff:
```python
import functools
import math

import jax
import jax.numpy as jnp
from jax import lax
from jax.experimental import pallas as pl
from jax.experimental.pallas import tpu as pltpu
from jax.sharding import PartitionSpec as P

HQ = 64
KVH = 8
CHUNKS = 2
MASKED_SCORE = -1e30
FLOOR = -1e29
MESH = pl.DeviceIdType.MESH


def slot_table(head_of_slot):
    slot_total = head_of_slot.shape[0]
    slot_ids = jnp.arange(slot_total, dtype=jnp.int32)
    return jnp.sum(
        jnp.where(head_of_slot[None, :] == slot_ids[:, None], slot_ids[None, :], 0), axis=1
    )


def greet(axes):
    barrier = pltpu.get_barrier_semaphore()
    total = 0
    for axis in axes:
        n = lax.axis_size(axis)
        me = lax.axis_index(axis)
        for k in range(1, n):
            pl.semaphore_signal(
                barrier, inc=1, device_id={axis: lax.rem(me + k, n)}, device_id_type=MESH
            )
            total += 1
    pl.semaphore_wait(barrier, total)


def remote(src, dst, send_sem, recv_sem, axis, k):
    n = lax.axis_size(axis)
    target = lax.rem(lax.axis_index(axis) + k, n)
    return pltpu.make_async_remote_copy(
        src_ref=src,
        dst_ref=dst,
        send_sem=send_sem,
        recv_sem=recv_sem,
        device_id={axis: target},
        device_id_type=MESH,
    )


def back(axis, index):
    n = lax.axis_size(axis)
    return lax.rem(lax.axis_index(axis) + n - index, n)


def gather_attend_kernel(
    dims, hos, lens, q_ref, kv_ref, att_ref,
    zq, xs, xr, osend, orecv, lsend, lrecv, scores,
    zq_s, zq_r, xq_s, xq_r, o_s, o_r, l_s, l_r, own_sem,
):
    nc, bq, nsq, hl, ns, per_tp, Lb, hd, G, T = dims
    n_tp, n_seq = lax.axis_size("tp"), lax.axis_size("seq")
    me_t, me_s = lax.axis_index("tp"), lax.axis_index("seq")
    rows = G * T
    block = math.gcd(Lb, 256)
    scale = math.log2(math.e) / math.sqrt(hd)
    greet(("tp", "seq"))

    zsends = [
        [remote(q_ref.at[c], zq[c].at[k], zq_s.at[c, k], zq_r.at[c, k], "tp", k) for k in range(1, n_tp)]
        for c in range(nc)
    ]
    owns = [pltpu.make_async_copy(q_ref.at[c], zq[c].at[0], own_sem.at[c]) for c in range(nc)]
    for c in range(nc):
        for copy in zsends[c]:
            copy.start()
        owns[c].start()

    xsends = [
        [remote(xs.at[c, k], xr.at[c, k], xq_s.at[c, k], xq_r.at[c, k], "seq", k) for k in range(1, n_seq)]
        for c in range(nc)
    ]

    def spread(c):
        owns[c].wait()
        for copy in zsends[c]:
            copy.wait_recv()
        for k in list(range(1, n_seq)) + [0]:
            target = xr if k == 0 else xs
            column = lax.rem(me_s + k, n_seq)
            for j in range(ns):
                head = hos[column * ns + j]
                target[c, k, j] = zq[c][back("tp", head // hl), head % hl]
            if k:
                xsends[c][k - 1].start()

    osends = [
        [remote(osend.at[c, k], orecv.at[c, k], o_s.at[c, k], o_r.at[c, k], "tp", k) for k in range(1, n_tp)]
        for c in range(nc)
    ]
    lsends = [
        [remote(lsend.at[c, k], lrecv.at[c, k], l_s.at[c, k], l_r.at[c, k], "tp", k) for k in range(1, n_tp)]
        for c in range(nc)
    ]

    def attend_pair(c, k, pair):
        x, slot = pair // ns, pair % ns
        plane = lax.rem(me_t + k, n_tp)
        local_seq = plane * bq + x
        whole_seq = plane * per_tp + c * bq + x
        source = back("seq", local_seq // nsq)
        queries = xr[c, source, slot, local_seq % nsq].reshape(rows, hd)
        visible_end = lens[whole_seq] - me_t * Lb
        limits = visible_end - T + lax.broadcasted_iota(jnp.int32, (1, rows), 1) % T
        top = jnp.full((1, rows), FLOOR, jnp.float32)
        for i in range(Lb // block):
            s = lax.dot_general(
                kv_ref[slot, whole_seq, i * block : (i + 1) * block, :hd],
                queries,
                (((1,), (1,)), ((), ())),
                preferred_element_type=jnp.float32,
            )
            pos = i * block + lax.broadcasted_iota(jnp.int32, (block, 1), 0)
            s = jnp.where(pos <= limits, s * scale, MASKED_SCORE)
            scores[i * block : (i + 1) * block, :] = s
            top = jnp.maximum(top, jnp.max(s, axis=0, keepdims=True))
        total = jnp.zeros((1, rows), jnp.float32)
        out = jnp.zeros((hd, rows), jnp.float32)
        for i in range(Lb // block):
            w = jnp.exp2(scores[i * block : (i + 1) * block, :] - top)
            total = total + jnp.sum(w, axis=0, keepdims=True)
            out = out + lax.dot_general(
                kv_ref[slot, whole_seq, i * block : (i + 1) * block, hd:],
                w.astype(jnp.bfloat16),
                (((0,), (0,)), ((), ())),
                preferred_element_type=jnp.float32,
            )
        total = jnp.maximum(total, 1e-30)
        o_to, l_to = (orecv, lrecv) if k == 0 else (osend, lsend)
        o_to[c, k, x, slot] = (out / total).astype(jnp.bfloat16)
        l_to[c, k, x, slot] = top + jnp.log2(total)

    def attend(c):
        for copy in xsends[c]:
            copy.wait_recv()
        order = sorted(range(1, n_tp), key=lambda k: abs(k - n_tp / 2)) + [0]
        for k in order:
            lax.fori_loop(0, bq * ns, lambda pair, _: (attend_pair(c, k, pair), 0)[1], 0)
            if k:
                osends[c][k - 1].start()
                lsends[c][k - 1].start()

    def merge(c):
        for k in range(n_tp - 1):
            osends[c][k].wait_recv()
            lsends[c][k].wait_recv()

        def one(pair, _):
            x, slot = pair // ns, pair % ns
            ls = [lrecv[c, k, x, slot] for k in range(n_tp)]
            top = functools.reduce(jnp.maximum, ls)
            ws = [jnp.exp2(l - top) for l in ls]
            inverse = 1.0 / sum(ws)
            out = jnp.zeros((hd, rows), jnp.float32)
            for k in range(n_tp):
                out = out + (ws[k] * inverse) * orecv[c, k, x, slot].astype(jnp.float32)
            att_ref[c, x, slot] = out.astype(jnp.bfloat16)
            return 0

        lax.fori_loop(0, bq * ns, one, 0)

    for c in range(nc):
        spread(c)
        if c:
            attend(c - 1)
    attend(nc - 1)
    for c in range(nc):
        merge(c)
    for c in range(nc):
        for copy in zsends[c] + xsends[c] + osends[c] + lsends[c]:
            copy.wait_send()


def gather_attend(qm, kv, head_of_slot, lengths, dims):
    nc, bq, nsq, hl, ns, per_tp, Lb, hd, G, T = dims
    n_tp, n_seq = lax.axis_size("tp"), lax.axis_size("seq")
    rows = G * T
    bf, f32 = jnp.bfloat16, jnp.float32
    dma = pltpu.SemaphoreType.DMA
    vmem = pl.BlockSpec(memory_space=pltpu.VMEM)
    smem = pl.BlockSpec(memory_space=pltpu.SMEM)
    return pl.pallas_call(
        functools.partial(gather_attend_kernel, dims),
        out_shape=jax.ShapeDtypeStruct((nc, bq, ns, hd, rows), bf),
        in_specs=[smem, smem, vmem, vmem],
        out_specs=vmem,
        scratch_shapes=[
            [pltpu.VMEM((n_tp, hl, nsq, G, T, hd), bf)] * nc,
            pltpu.VMEM((nc, n_seq, ns, nsq, G, T, hd), bf),
            pltpu.VMEM((nc, n_seq, ns, nsq, G, T, hd), bf),
            pltpu.VMEM((nc, n_tp, bq, ns, hd, rows), bf),
            pltpu.VMEM((nc, n_tp, bq, ns, hd, rows), bf),
            pltpu.VMEM((nc, n_tp, bq, ns, 1, rows), f32),
            pltpu.VMEM((nc, n_tp, bq, ns, 1, rows), f32),
            pltpu.VMEM((Lb, rows), f32),
            dma((nc, n_tp)), dma((nc, n_tp)), dma((nc, n_seq)), dma((nc, n_seq)),
            dma((nc, n_tp)), dma((nc, n_tp)), dma((nc, n_tp)), dma((nc, n_tp)), dma((nc,)),
        ],
        compiler_params=pltpu.CompilerParams(
            collective_id=0, has_side_effects=True, vmem_limit_bytes=56 * 2**20
        ),
    )(head_of_slot, lengths, qm, kv)


def project_kernel(
    dims, soh, att_ref, w_hbm, out_ref,
    w_ref, xr, zs, zr, ag, own, ps, pr,
    x_s, x_r, z_s, z_r, a_s, a_r, p_s, p_r, w_sem, own_sem,
):
    nc, bq, hl, ns, sub, part, T = dims
    n_tp, n_seq = lax.axis_size("tp"), lax.axis_size("seq")
    me_t, me_s = lax.axis_index("tp"), lax.axis_index("seq")
    width, columns = w_ref.shape
    few = bq * sub
    load = pltpu.make_async_copy(w_hbm, w_ref, w_sem)
    greet(("tp", "seq"))
    xsends = [
        [
            remote(att_ref.at[c, lax.rem(me_s + k, n_seq)], xr[c].at[k], x_s.at[c, k], x_r.at[c, k], "seq", k)
            for k in range(1, n_seq)
        ]
        for c in range(nc)
    ]
    owns = [pltpu.make_async_copy(att_ref.at[c, me_s], xr[c].at[0], own_sem.at[c]) for c in range(nc)]
    for c in range(nc):
        for copy in xsends[c]:
            copy.start()
        owns[c].start()
    load.start()
    zsends = [
        [remote(zs.at[c, k], zr.at[c, k], z_s.at[c, k], z_r.at[c, k], "tp", k) for k in range(1, n_tp)]
        for c in range(nc)
    ]
    asends = [
        [remote(zr.at[c], ag.at[c, k], a_s.at[c, k], a_r.at[c, k], "seq", k) for k in range(1, n_seq)]
        for c in range(nc)
    ]
    psends = [
        [remote(ps.at[c, k], pr.at[c, k], p_s.at[c, k], p_r.at[c, k], "tp", k) for k in range(1, n_tp)]
        for c in range(nc)
    ]
    for c in range(nc):
        owns[c].wait()
        for copy in xsends[c]:
            copy.wait_recv()
        for k in list(range(1, n_tp)) + [0]:
            target = zr if k == 0 else zs
            plane = lax.rem(me_t + k, n_tp)
            for j in range(hl):
                slot = soh[plane * hl + j]
                picked = xr[c][back("seq", slot // ns), slot % ns]
                target[c, k, :, j * part : (j + 1) * part] = picked
            if k:
                zsends[c][k - 1].start()
    for c in range(nc):
        for copy in zsends[c]:
            copy.wait_recv()
        for copy in asends[c]:
            copy.start()
    load.wait()
    tile = math.gcd(columns, 512)
    for c in range(nc):
        for copy in asends[c]:
            copy.wait_recv()
        pieces = []
        for k in range(n_tp):
            j = (n_tp - k) % n_tp
            for p in range(n_seq):
                pieces.append(zr[c, j] if p == 0 else ag[c, p, j])
        rows = jnp.concatenate(pieces, axis=0)

        def column_tile(i, _):
            at = pl.ds(pl.multiple_of(i * tile, tile), tile)
            product = jnp.dot(rows, w_ref[:, at], preferred_element_type=jnp.float32)
            span = n_seq * few
            own[c, :, at] = product[:span]
            for k in range(1, n_tp):
                ps[c, k, :, at] = product[k * span : (k + 1) * span].astype(jnp.bfloat16)
            return 0

        lax.fori_loop(0, columns // tile, column_tile, 0)
        for copy in psends[c]:
            copy.start()
    for c in range(nc):
        for copy in psends[c]:
            copy.wait_recv()
        for p in range(n_seq):
            column = lax.rem(me_s + n_seq - p, n_seq)
            for x in range(bq):
                at = p * few + x * sub
                total = own[c, at : at + sub]
                for k in range(1, n_tp):
                    total = total + pr[c, k, at : at + sub].astype(jnp.float32)
                out_ref[c * bq + x, pl.ds(pl.multiple_of(column * sub, sub), sub)] = total.astype(jnp.bfloat16)
    for c in range(nc):
        for copy in xsends[c] + zsends[c] + asends[c] + psends[c]:
            copy.wait_send()


def project(att, weight, slot_of_head, dims):
    nc, bq, hl, ns, sub, part, T = dims
    n_tp, n_seq = lax.axis_size("tp"), lax.axis_size("seq")
    width, columns = weight.shape
    few = bq * sub
    bf, f32 = jnp.bfloat16, jnp.float32
    dma = pltpu.SemaphoreType.DMA
    vmem = pl.BlockSpec(memory_space=pltpu.VMEM)
    return pl.pallas_call(
        functools.partial(project_kernel, dims),
        out_shape=jax.ShapeDtypeStruct((nc * bq, T, columns), bf),
        in_specs=[
            pl.BlockSpec(memory_space=pltpu.SMEM), vmem, pl.BlockSpec(memory_space=pl.ANY)
        ],
        out_specs=vmem,
        scratch_shapes=[
            pltpu.VMEM((width, columns), bf),
            [pltpu.VMEM((n_seq, ns, few, part), bf)] * nc,
            pltpu.VMEM((nc, n_tp, few, width), bf),
            pltpu.VMEM((nc, n_tp, few, width), bf),
            pltpu.VMEM((nc, n_seq, n_tp, few, width), bf),
            pltpu.VMEM((nc, n_seq * few, columns), f32),
            pltpu.VMEM((nc, n_tp, n_seq * few, columns), bf),
            pltpu.VMEM((nc, n_tp, n_seq * few, columns), bf),
            dma((nc, n_seq)), dma((nc, n_seq)), dma((nc, n_tp)), dma((nc, n_tp)),
            dma((nc, n_seq)), dma((nc, n_seq)), dma((nc, n_tp)), dma((nc, n_tp)),
            dma(()), dma((nc,)),
        ],
        compiler_params=pltpu.CompilerParams(
            collective_id=1, has_side_effects=True, vmem_limit_bytes=48 * 2**20
        ),
    )(slot_of_head, att, weight)


def local(query, cache, head_of_slot, lengths, out_weight):
    G = HQ // KVH
    n_seq, n_tp = lax.axis_size("seq"), lax.axis_size("tp")
    me_s = lax.axis_index("seq")
    slot_of_head = slot_table(head_of_slot)
    B, T, width = query.shape
    Lb, ns, hd2 = cache.shape[1:]
    hd = hd2 // 2
    hl = KVH // n_tp
    per_tp = B // n_tp
    nc = math.gcd(CHUNKS, per_tp)
    bq = per_tp // nc
    nsq = n_tp * bq // n_seq
    sub = T // n_seq

    chunked = query.reshape(n_tp, nc, bq, T, width).transpose(1, 0, 2, 3, 4)
    chunked = chunked.reshape(nc, n_seq, nsq, T, width)
    mine = lax.dynamic_index_in_dim(chunked, me_s, 1, False)
    qm = mine.reshape(nc, nsq, T, hl, G, hd).transpose(0, 3, 1, 4, 2, 5)
    kv = cache.transpose(2, 0, 1, 3)
    att = gather_attend(
        qm, kv, head_of_slot, lengths, (nc, bq, nsq, hl, ns, per_tp, Lb, hd, G, T)
    )
    att = att.reshape(nc, bq, ns, hd, G, n_seq, sub).transpose(0, 5, 2, 1, 6, 4, 3)
    att = att.reshape(nc, n_seq, ns, bq * sub, G * hd)
    return project(att, out_weight, slot_of_head, (nc, bq, hl, ns, sub, G * hd, T))


def solution(mesh):
    in_specs = (
        P("grp", None, "tp"),
        P("grp", "tp", "seq", None),
        P("grp"),
        P("grp"),
        P("tp", "seq"),
    )
    out_specs = P(("grp", "tp"), None, "seq")
    return jax.shard_map(local, mesh=mesh, in_specs=in_specs, out_specs=out_specs, check_vma=False)
```

time: 706 us -> 184 us (0.26)
  waiting for transfers between devices: 487 us -> 0 us
  Pallas kernels: 0 us -> 170 us
  matrix products: 58.8 us -> 0 us
  other arithmetic: 55.8 us -> 0.12 us
  local copies, waits for them, and re-layouts: 58 us -> 13.4 us
  blocking collectives: 17 us -> 0 us
  between operations: 13.5 us -> 0.06 us
  starting transfers between devices: 12.3 us -> 0 us
    all_to_all x2 -> x0, waiting for transfers between devices: 270 us -> none  [the longest x1 178 us: local(): lax.all_to_all(by_head, 'tp', split_axis=2, concat_axis=1, tiled=True)]
    pallas_call x0 -> x2, Pallas kernels: none -> 170 us  [the longest x1 94.7 us: gather_attend(): pl.pallas_call(functools.partial(gather_attend_kernel, dims), out_shape=j...]
    all_gather x1 -> x0, waiting for transfers between devices: 141 us -> none  [merged(): everything = jax.tree.map(lambda part: lax.all_gather(part, axis), shard)]
    reduce_scatter x1 -> x0, waiting for transfers between devices: 76.4 us -> none  [local(): lax.psum_scatter(jnp.dot(flattened, out_weight, preferred_element_type=jn...]
    dot_general x5 -> x0, matrix products: 58.8 us -> none  [the longest x2 25.4 us: advance(): jnp.einsum('bnrk,bknd->bnrd', weights.astype(jnp.bfloat16), entry_block[....]
    all_to_all x4 -> x0, local copies, waits for them, and re-layouts: 32.4 us -> none  [the longest x3 24.8 us: local(): lax.all_to_all(cache, 'seq', split_axis=1, concat_axis=2, tiled=True)]
    add x11 -> x0, other arithmetic: 24.4 us -> none  [the longest x3 23.9 us: combine(): earlier[2] * early_scale[..., None] + latter[2] * late_scale[..., None]]
    all_gather x2 -> x0, blocking collectives: 17 us -> none  [merged(): everything = jax.tree.map(lambda part: lax.all_gather(part, axis), shard)]
  transfers between devices with their start and end apart: 4 -> 0, of which waited for: 4 -> 0; matrix products, arithmetic and copies ran while one was open for 0% -> 0% of each run, Pallas kernels for 0% -> 0%
where the time goes in v1:
time: 184 us; the launch traced here: 183 us
  Pallas kernels  170 us (92%)
  local copies, waits for them, and re-layouts  13.4 us (7%)
    pallas_call x1, Pallas kernels, gather_attend(): pl.pallas_call(functools.partial(gather_attend_kernel, dims), out_shape=j...  94.7 us
    pallas_call x1, Pallas kernels, project(): pl.pallas_call(functools.partial(project_kernel, dims), out_shape=jax.Sha...  75.2 us
    unnamed x7, local copies, waits for them, and re-layouts  10.5 us

profile of v1, /device:TPU:28, one launch (start us, length us, event | category | flops | bytes accessed | tf_op | source)
XLA Modules:
  0.0 183.4 jit_solution(12680813287602147725)
XLA Ops:
  0.0 0.0 copy-start
  0.0 1.6 copy-done
  1.6 0.1 copy.18
  1.8 0.9 copy.22
  2.7 8.0 %copy.21 = bf16[8,1024,2,256]{3,1,0,2:T(8,128)(2,1)} copy(bf16[8,1024,2,256]{3,2,1,0:T(2,128)(2,1)} %param.6) | data formatting | bytes 16777216 | tf_op args[1]
  10.7 0.0 copy-start.1
  10.7 94.7 %shard_map.55 = bf16[2,1,2,128,512]{4,3,2,1,0:T(8,128)(2,1)} custom-call(s32[8]{0:T(128)} %hos.1, s32[8]{0:T(128)} %lens.1, bf16[2,2,1,8,64,128]{5,4,3,2,1,0:T(8,128)(2,1)} %bitcast.25, bf16[2,8,1024,256]{3,2,1,0:T(8,128)(2,1)} %bitcast.24), custom_call_target="tpu_custom_call" | custom-call | tf_op jit(solution)/shard_map/pallas_call | solution.py:195
  105.4 1.3 copy.16
  106.7 0.3 copy.17
  107.1 0.2 reshape.19.att_ref
  107.3 0.0 copy-done.1
  107.3 0.1 select_reduce_fusion.soh
  107.4 75.2 %shard_map.56 = bf16[2,64,2048]{2,1,0:T(8,128)(2,1)S(1)} custom-call(s32[8]{0:T(128)S(1)} %select_reduce_fusion.soh, bf16[2,4,2,16,1024]{4,3,2,1,0:T(8,128)(2,1)S(1)} %reshape.19.att_ref, bf16[2048,2048]{1,0:T(8,128)(2,1)} %w_hbm.1), custom_call_target="tpu_custom_call" | custom-call | tf_op jit(solution)/shard_map/pallas_call | solution.py:321
  182.6 0.8 copy.24
  (1 shorter events, 0.0 us)
Async XLA Ops:
  0.0 1.6 copy-start
  10.7 96.6 %copy-start.1 = (s32[8]{0:T(128)S(1)}, s32[8]{0:T(128)}, u32[]{:S(2)}) copy-start(s32[8]{0:T(128)} %hos.1) | copy-start | bytes 100

commit v2 on v1

v2 whole, which is shorter than its diff:
```python
import functools
import math

import jax
import jax.numpy as jnp
from jax import lax
from jax.experimental import pallas as pl
from jax.experimental.pallas import tpu as pltpu
from jax.sharding import PartitionSpec as P

HQ = 64
KVH = 8
CHUNKS = 2
MASKED_SCORE = -1e30
FLOOR = -1e29
MESH = pl.DeviceIdType.MESH


def slot_table(head_of_slot):
    slot_total = head_of_slot.shape[0]
    slot_ids = jnp.arange(slot_total, dtype=jnp.int32)
    return jnp.sum(
        jnp.where(head_of_slot[None, :] == slot_ids[:, None], slot_ids[None, :], 0), axis=1
    )


def greet(axes):
    barrier = pltpu.get_barrier_semaphore()
    total = 0
    for axis in axes:
        n = lax.axis_size(axis)
        me = lax.axis_index(axis)
        for k in range(1, n):
            pl.semaphore_signal(
                barrier, inc=1, device_id={axis: lax.rem(me + k, n)}, device_id_type=MESH
            )
            total += 1
    pl.semaphore_wait(barrier, total)


def remote(src, dst, send_sem, recv_sem, axis, k):
    n = lax.axis_size(axis)
    target = lax.rem(lax.axis_index(axis) + k, n)
    return pltpu.make_async_remote_copy(
        src_ref=src,
        dst_ref=dst,
        send_sem=send_sem,
        recv_sem=recv_sem,
        device_id={axis: target},
        device_id_type=MESH,
    )


def back(axis, index):
    n = lax.axis_size(axis)
    return lax.rem(lax.axis_index(axis) + n - index, n)


def layer_kernel(
    dims, hos, soh, lens, q_ref, kv_ref, w_hbm, out_ref,
    zq, xs, xr, osend, orecv, lsend, lrecv, scores,
    zq_s, zq_r, xq_s, xq_r, o_s, o_r, l_s, l_r, own_sem,
    att, w_ref, xa, zs, zr, ag, own, ps, pr,
    x_s, x_r, z_s, z_r, a_s, a_r, p_s, p_r, w_sem,
):
    nc, bq, nsq, hl, ns, per_tp, Lb, hd, G, T = dims
    width, columns = w_ref.shape
    sub = T // lax.axis_size("seq")
    few = bq * sub
    part = G * hd
    load = pltpu.make_async_copy(w_hbm, w_ref, w_sem)
    n_tp, n_seq = lax.axis_size("tp"), lax.axis_size("seq")
    me_t, me_s = lax.axis_index("tp"), lax.axis_index("seq")
    rows = G * T
    block = math.gcd(Lb, 256)
    scale = math.log2(math.e) / math.sqrt(hd)
    greet(("tp", "seq"))

    zsends = [
        [remote(q_ref.at[c], zq[c].at[k], zq_s.at[c, k], zq_r.at[c, k], "tp", k) for k in range(1, n_tp)]
        for c in range(nc)
    ]
    owns = [pltpu.make_async_copy(q_ref.at[c], zq[c].at[0], own_sem.at[c]) for c in range(nc)]
    for c in range(nc):
        for copy in zsends[c]:
            copy.start()
        owns[c].start()

    xsends = [
        [remote(xs.at[c, k], xr.at[c, k], xq_s.at[c, k], xq_r.at[c, k], "seq", k) for k in range(1, n_seq)]
        for c in range(nc)
    ]

    def spread(c):
        owns[c].wait()
        for copy in zsends[c]:
            copy.wait_recv()
        for k in list(range(1, n_seq)) + [0]:
            target = xr if k == 0 else xs
            column = lax.rem(me_s + k, n_seq)
            for j in range(ns):
                head = hos[column * ns + j]
                target[c, k, j] = zq[c][back("tp", head // hl), head % hl]
            if k:
                xsends[c][k - 1].start()

    osends = [
        [remote(osend.at[c, k], orecv.at[c, k], o_s.at[c, k], o_r.at[c, k], "tp", k) for k in range(1, n_tp)]
        for c in range(nc)
    ]
    lsends = [
        [remote(lsend.at[c, k], lrecv.at[c, k], l_s.at[c, k], l_r.at[c, k], "tp", k) for k in range(1, n_tp)]
        for c in range(nc)
    ]

    def attend_pair(c, k, pair):
        x, slot = pair // ns, pair % ns
        plane = lax.rem(me_t + k, n_tp)
        local_seq = plane * bq + x
        whole_seq = plane * per_tp + c * bq + x
        source = back("seq", local_seq // nsq)
        queries = xr[c, source, slot, local_seq % nsq].reshape(rows, hd)
        visible_end = lens[whole_seq] - me_t * Lb
        limits = visible_end - T + lax.broadcasted_iota(jnp.int32, (1, rows), 1) % T
        top = jnp.full((1, rows), FLOOR, jnp.float32)
        for i in range(Lb // block):
            s = lax.dot_general(
                kv_ref[slot, whole_seq, i * block : (i + 1) * block, :hd],
                queries,
                (((1,), (1,)), ((), ())),
                preferred_element_type=jnp.float32,
            )
            pos = i * block + lax.broadcasted_iota(jnp.int32, (block, 1), 0)
            s = jnp.where(pos <= limits, s * scale, MASKED_SCORE)
            scores[i * block : (i + 1) * block, :] = s
            top = jnp.maximum(top, jnp.max(s, axis=0, keepdims=True))
        total = jnp.zeros((1, rows), jnp.float32)
        out = jnp.zeros((hd, rows), jnp.float32)
        for i in range(Lb // block):
            w = jnp.exp2(scores[i * block : (i + 1) * block, :] - top)
            total = total + jnp.sum(w, axis=0, keepdims=True)
            out = out + lax.dot_general(
                kv_ref[slot, whole_seq, i * block : (i + 1) * block, hd:],
                w.astype(jnp.bfloat16),
                (((0,), (0,)), ((), ())),
                preferred_element_type=jnp.float32,
            )
        total = jnp.maximum(total, 1e-30)
        o_to, l_to = (orecv, lrecv) if k == 0 else (osend, lsend)
        o_to[c, k, x, slot] = (out / total).astype(jnp.bfloat16)
        l_to[c, k, x, slot] = top + jnp.log2(total)

    def attend(c):
        for copy in xsends[c]:
            copy.wait_recv()
        order = sorted(range(1, n_tp), key=lambda k: abs(k - n_tp / 2)) + [0]
        for k in order:
            lax.fori_loop(0, bq * ns, lambda pair, _: (attend_pair(c, k, pair), 0)[1], 0)
            if k:
                osends[c][k - 1].start()
                lsends[c][k - 1].start()

    asends = [
        [remote(zr.at[c], ag.at[c, k], a_s.at[c, k], a_r.at[c, k], "seq", k) for k in range(1, n_seq)]
        for c in range(nc)
    ]
    rsends = [
        [
            remote(att.at[c, lax.rem(me_s + k, n_seq)], xa[c].at[k], x_s.at[c, k], x_r.at[c, k], "seq", k)
            for k in range(1, n_seq)
        ]
        for c in range(nc)
    ]
    psends = [
        [remote(ps.at[c, k], pr.at[c, k], p_s.at[c, k], p_r.at[c, k], "tp", k) for k in range(1, n_tp)]
        for c in range(nc)
    ]
    hsends = [
        [remote(zs.at[c, k], zr.at[c, k], z_s.at[c, k], z_r.at[c, k], "tp", k) for k in range(1, n_tp)]
        for c in range(nc)
    ]
    keeps = [pltpu.make_async_copy(att.at[c, me_s], xa[c].at[0], own_sem.at[nc + c]) for c in range(nc)]

    def merge(c):
        for k in range(n_tp - 1):
            osends[c][k].wait_recv()
            lsends[c][k].wait_recv()
        for pair in range(bq * ns):
            x, slot = pair // ns, pair % ns
            ls = [lrecv[c, k, x, slot] for k in range(n_tp)]
            top = functools.reduce(jnp.maximum, ls)
            ws = [jnp.exp2(l - top) for l in ls]
            inverse = 1.0 / sum(ws)
            out = jnp.zeros((hd, rows), jnp.float32)
            for k in range(n_tp):
                out = out + (ws[k] * inverse) * orecv[c, k, x, slot].astype(jnp.float32)
            out = out.T.astype(jnp.bfloat16)
            for p in range(n_seq):
                for g in range(G):
                    at = g * T + p * sub
                    att[c, p, slot, x * sub : (x + 1) * sub, g * hd : (g + 1) * hd] = out[at : at + sub]
        for copy in rsends[c]:
            copy.start()
        keeps[c].start()

    def to_planes(c):
        keeps[c].wait()
        for copy in rsends[c]:
            copy.wait_recv()
        for k in list(range(1, n_tp)) + [0]:
            target = zr if k == 0 else zs
            plane = lax.rem(me_t + k, n_tp)
            for j in range(hl):
                slot = soh[plane * hl + j]
                picked = xa[c][back("seq", slot // ns), slot % ns]
                target[c, k, :, j * part : (j + 1) * part] = picked
            if k:
                hsends[c][k - 1].start()

    def to_columns(c):
        for copy in hsends[c]:
            copy.wait_recv()
        for copy in asends[c]:
            copy.start()

    tile = math.gcd(columns, 512)
    span = n_seq * few

    def multiply(c):
        for copy in asends[c]:
            copy.wait_recv()
        pieces = []
        for k in range(n_tp):
            j = (n_tp - k) % n_tp
            for p in range(n_seq):
                pieces.append(zr[c, j] if p == 0 else ag[c, p, j])
        left = jnp.concatenate(pieces, axis=0)

        def column_tile(i, _):
            at = pl.ds(pl.multiple_of(i * tile, tile), tile)
            product = jnp.dot(left, w_ref[:, at], preferred_element_type=jnp.float32)
            own[c, :, at] = product[:span]
            for k in range(1, n_tp):
                ps[c, k, :, at] = product[k * span : (k + 1) * span].astype(jnp.bfloat16)
            return 0

        lax.fori_loop(0, columns // tile, column_tile, 0)
        for copy in psends[c]:
            copy.start()

    def finish(c):
        for copy in psends[c]:
            copy.wait_recv()
        for p in range(n_seq):
            column = lax.rem(me_s + n_seq - p, n_seq)
            for x in range(bq):
                at = p * few + x * sub
                total = own[c, at : at + sub]
                for k in range(1, n_tp):
                    total = total + pr[c, k, at : at + sub].astype(jnp.float32)
                out_ref[c * bq + x, pl.ds(pl.multiple_of(column * sub, sub), sub)] = total.astype(jnp.bfloat16)

    load.start()
    for c in range(nc):
        spread(c)
        attend(c)
        if c:
            merge(c - 1)
            to_planes(c - 1)
    load.wait()
    for c in range(nc):
        if c:
            to_columns(c - 1)
        if c == nc - 1:
            merge(c)
            to_planes(c)
        if c:
            multiply(c - 1)
        if c == nc - 1:
            to_columns(c)
            multiply(c)
    for c in range(nc):
        finish(c)
    for c in range(nc):
        for copy in (
            zsends[c] + xsends[c] + osends[c] + lsends[c] + rsends[c] + hsends[c] + asends[c] + psends[c]
        ):
            copy.wait_send()


def layer(qm, kv, weight, head_of_slot, slot_of_head, lengths, dims):
    nc, bq, nsq, hl, ns, per_tp, Lb, hd, G, T = dims
    n_tp, n_seq = lax.axis_size("tp"), lax.axis_size("seq")
    rows = G * T
    width, columns = weight.shape
    sub = T // n_seq
    few = bq * sub
    bf, f32 = jnp.bfloat16, jnp.float32
    dma = pltpu.SemaphoreType.DMA
    vmem = pl.BlockSpec(memory_space=pltpu.VMEM)
    smem = pl.BlockSpec(memory_space=pltpu.SMEM)
    tp_sem, seq_sem = dma((nc, n_tp)), dma((nc, n_seq))
    return pl.pallas_call(
        functools.partial(layer_kernel, dims),
        out_shape=jax.ShapeDtypeStruct((nc * bq, T, columns), bf),
        in_specs=[smem, smem, smem, vmem, vmem, pl.BlockSpec(memory_space=pl.ANY)],
        out_specs=vmem,
        scratch_shapes=[
            [pltpu.VMEM((n_tp, hl, nsq, G, T, hd), bf)] * nc,
            pltpu.VMEM((nc, n_seq, ns, nsq, G, T, hd), bf),
            pltpu.VMEM((nc, n_seq, ns, nsq, G, T, hd), bf),
            pltpu.VMEM((nc, n_tp, bq, ns, hd, rows), bf),
            pltpu.VMEM((nc, n_tp, bq, ns, hd, rows), bf),
            pltpu.VMEM((nc, n_tp, bq, ns, 1, rows), f32),
            pltpu.VMEM((nc, n_tp, bq, ns, 1, rows), f32),
            pltpu.VMEM((Lb, rows), f32),
            tp_sem, tp_sem, seq_sem, seq_sem, tp_sem, tp_sem, tp_sem, tp_sem, dma((2 * nc,)),
            pltpu.VMEM((nc, n_seq, ns, few, G * hd), bf),
            pltpu.VMEM((width, columns), bf),
            [pltpu.VMEM((n_seq, ns, few, G * hd), bf)] * nc,
            pltpu.VMEM((nc, n_tp, few, width), bf),
            pltpu.VMEM((nc, n_tp, few, width), bf),
            pltpu.VMEM((nc, n_seq, n_tp, few, width), bf),
            pltpu.VMEM((nc, n_seq * few, columns), f32),
            pltpu.VMEM((nc, n_tp, n_seq * few, columns), bf),
            pltpu.VMEM((nc, n_tp, n_seq * few, columns), bf),
            seq_sem, seq_sem, tp_sem, tp_sem, seq_sem, seq_sem, tp_sem, tp_sem, dma(()),
        ],
        compiler_params=pltpu.CompilerParams(
            collective_id=0, has_side_effects=True, vmem_limit_bytes=58 * 2**20
        ),
    )(head_of_slot, slot_of_head, lengths, qm, kv, weight)


def local(query, cache, head_of_slot, lengths, out_weight):
    G = HQ // KVH
    n_seq, n_tp = lax.axis_size("seq"), lax.axis_size("tp")
    me_s = lax.axis_index("seq")
    slot_of_head = slot_table(head_of_slot)
    B, T, width = query.shape
    Lb, ns, hd2 = cache.shape[1:]
    hd = hd2 // 2
    hl = KVH // n_tp
    per_tp = B // n_tp
    nc = math.gcd(CHUNKS, per_tp)
    bq = per_tp // nc
    nsq = n_tp * bq // n_seq

    chunked = query.reshape(n_tp, nc, bq, T, width).transpose(1, 0, 2, 3, 4)
    chunked = chunked.reshape(nc, n_seq, nsq, T, width)
    mine = lax.dynamic_index_in_dim(chunked, me_s, 1, False)
    qm = mine.reshape(nc, nsq, T, hl, G, hd).transpose(0, 3, 1, 4, 2, 5)
    kv = cache.transpose(2, 0, 1, 3)
    dims = (nc, bq, nsq, hl, ns, per_tp, Lb, hd, G, T)
    return layer(qm, kv, out_weight, head_of_slot, slot_of_head, lengths, dims)


def solution(mesh):
    in_specs = (
        P("grp", None, "tp"),
        P("grp", "tp", "seq", None),
        P("grp"),
        P("grp"),
        P("tp", "seq"),
    )
    out_specs = P(("grp", "tp"), None, "seq")
    return jax.shard_map(local, mesh=mesh, in_specs=in_specs, out_specs=out_specs, check_vma=False)
```

time: 184 us -> 188 us (1.022)
  Pallas kernels: 170 us -> 173 us
    pallas_call x2 -> x1, Pallas kernels: 170 us -> 173 us  [layer(): pl.pallas_call(functools.partial(layer_kernel, dims), out_shape=jax.Shape...]
    unnamed x7 -> x5, local copies, waits for them, and re-layouts: 10.5 us -> 11.6 us
where the time goes in v2:
time: 188 us; the launch traced here: 187 us
  Pallas kernels  173 us (92%)
  local copies, waits for them, and re-layouts  12.6 us (7%)
    pallas_call x1, Pallas kernels, layer(): pl.pallas_call(functools.partial(layer_kernel, dims), out_shape=jax.Shape...  173 us
    unnamed x5, local copies, waits for them, and re-layouts  11.6 us

profile of v2, /device:TPU:28, one launch (start us, length us, event | category | flops | bytes accessed | tf_op | source)
XLA Modules:
  0.0 187.2 jit_solution(5960444185811071855)
XLA Ops:
  0.0 0.0 copy-start
  0.0 1.6 copy-done
  1.6 1.3 select_reduce_fusion.soh
  2.9 0.1 copy.13
  3.1 0.9 copy.17
  4.0 8.0 %copy.16 = bf16[8,1024,2,256]{3,1,0,2:T(8,128)(2,1)} copy(bf16[8,1024,2,256]{3,2,1,0:T(2,128)(2,1)} %param.6) | data formatting | bytes 16777216 | tf_op args[1]
  12.0 173.3 %shard_map.55 = bf16[2,64,2048]{2,1,0:T(8,128)(2,1)} custom-call(s32[8]{0:T(128)} %hos.1, s32[8]{0:T(128)} %select_reduce_fusion.soh, s32[8]{0:T(128)} %lens.1, bf16[2,2,1,8,64,128]{5,4,3,2,1,0:T(8,128)(2,1)} %bitcast.18, bf16[2,8,1024,256]{3,2,1,0:T(8,128)(2,1)} %bitcast.17, bf16[2048,2048]{1,0:T(8,128)(2,1)} %w_hbm.1), custom_call_target="tpu_custom_call" | custom-call | tf_op jit(solution)/shard_map/pallas_call | solution.py:303
  185.3 1.9 %copy.19 = bf16[2,64,2048]{2,1,0:T(8,128)(2,1)} copy(bf16[2,64,2048]{2,1,0:T(8,128)(2,1)} %shard_map.55) | data formatting | bytes 1048576
  (1 shorter events, 0.0 us)
Async XLA Ops:
  0.0 1.6 copy-start

commit v3 on v1

--- a/solution.py
+++ b/solution.py
@@ -57,8 +57,8 @@
 
 
 def gather_attend_kernel(
-    dims, hos, lens, q_ref, kv_ref, att_ref,
-    zq, xs, xr, osend, orecv, lsend, lrecv, scores,
+    dims, hos, lens, q_ref, kv_hbm, att_ref,
+    raw, kv_ref, kv_sem, zq, xs, xr, osend, orecv, lsend, lrecv, scores,
     zq_s, zq_r, xq_s, xq_r, o_s, o_r, l_s, l_r, own_sem,
 ):
     nc, bq, nsq, hl, ns, per_tp, Lb, hd, G, T = dims
@@ -67,6 +67,8 @@
     rows = G * T
     block = math.gcd(Lb, 256)
     scale = math.log2(math.e) / math.sqrt(hd)
+    fetch = pltpu.make_async_copy(kv_hbm, raw, kv_sem)
+    fetch.start()
     greet(("tp", "seq"))
 
     zsends = [
@@ -172,6 +174,17 @@
 
         lax.fori_loop(0, bq * ns, one, 0)
 
+    fetch.wait()
+    step = math.gcd(Lb, 128)
+    turns = Lb // step
+
+    def split(turn, _):
+        at = pl.ds(pl.multiple_of(turn % turns * step, step), step)
+        for slot in range(ns):
+            kv_ref[slot, turn // turns, at, :] = raw[turn // turns, at, slot, :]
+        return 0
+
+    lax.fori_loop(0, raw.shape[0] * turns, split, 0)
     for c in range(nc):
         spread(c)
         if c:
@@ -195,9 +208,12 @@
     return pl.pallas_call(
         functools.partial(gather_attend_kernel, dims),
         out_shape=jax.ShapeDtypeStruct((nc, bq, ns, hd, rows), bf),
-        in_specs=[smem, smem, vmem, vmem],
+        in_specs=[smem, smem, vmem, pl.BlockSpec(memory_space=pl.ANY)],
         out_specs=vmem,
         scratch_shapes=[
+            pltpu.VMEM(kv.shape, bf),
+            pltpu.VMEM((ns, kv.shape[0], Lb, 2 * hd), bf),
+            dma(()),
             [pltpu.VMEM((n_tp, hl, nsq, G, T, hd), bf)] * nc,
             pltpu.VMEM((nc, n_seq, ns, nsq, G, T, hd), bf),
             pltpu.VMEM((nc, n_seq, ns, nsq, G, T, hd), bf),
@@ -363,7 +379,7 @@
     chunked = chunked.reshape(nc, n_seq, nsq, T, width)
     mine = lax.dynamic_index_in_dim(chunked, me_s, 1, False)
     qm = mine.reshape(nc, nsq, T, hl, G, hd).transpose(0, 3, 1, 4, 2, 5)
-    kv = cache.transpose(2, 0, 1, 3)
+    kv = cache
     att = gather_attend(
         qm, kv, head_of_slot, lengths, (nc, bq, nsq, hl, ns, per_tp, Lb, hd, G, T)
     )

time: 184 us -> 174 us (0.946)
  local copies, waits for them, and re-layouts: 13.4 us -> 5.35 us
  Pallas kernels: 170 us -> 167 us
    unnamed x7 -> x4, local copies, waits for them, and re-layouts: 10.5 us -> 2.5 us
    pallas_call x1, Pallas kernels: 94.7 us -> 92.1 us  [gather_attend(): pl.pallas_call(functools.partial(gather_attend_kernel, dims), out_shape=j...]
where the time goes in v3:
time: 174 us
  Pallas kernels  167 us (96%)
  local copies, waits for them, and re-layouts  5.35 us (3%)
    pallas_call x1, Pallas kernels, gather_attend(): pl.pallas_call(functools.partial(gather_attend_kernel, dims), out_shape=j...  92.1 us
    pallas_call x1, Pallas kernels, project(): pl.pallas_call(functools.partial(project_kernel, dims), out_shape=jax.Sha...  75.2 us

profile of v3, /device:TPU:28, one launch (start us, length us, event | category | flops | bytes accessed | tf_op | source)
XLA Modules:
  0.0 173.6 jit_solution(11986243077703983417)
XLA Ops:
  0.0 0.0 copy-start
  0.0 1.6 copy-done
  1.6 0.8 select_reduce_fusion.soh
  2.4 0.1 copy.15
  2.5 0.9 copy.17
  3.5 92.1 %shard_map.55 = bf16[2,1,2,128,512]{4,3,2,1,0:T(8,128)(2,1)} custom-call(s32[8]{0:T(128)} %hos.1, s32[8]{0:T(128)} %lens.1, bf16[2,2,1,8,64,128]{5,4,3,2,1,0:T(8,128)(2,1)} %bitcast.21, bf16[8,1024,2,256]{3,2,1,0:T(2,128)(2,1)} %kv_hbm.1), custom_call_target="tpu_custom_call" | custom-call | tf_op jit(solution)/shard_map/pallas_call | solution.py:208
  95.6 1.3 copy.13
  96.9 0.3 copy.14
  97.3 0.2 reshape.19.att_ref
  97.5 75.2 %shard_map.56 = bf16[2,64,2048]{2,1,0:T(8,128)(2,1)S(1)} custom-call(s32[8]{0:T(128)S(1)} %select_reduce_fusion.soh, bf16[2,4,2,16,1024]{4,3,2,1,0:T(8,128)(2,1)S(1)} %reshape.19.att_ref, bf16[2048,2048]{1,0:T(8,128)(2,1)} %w_hbm.1), custom_call_target="tpu_custom_call" | custom-call | tf_op jit(solution)/shard_map/pallas_call | solution.py:337
  172.8 0.8 copy.19
  (1 shorter events, 0.0 us)
Async XLA Ops:
  0.0 1.6 copy-start
